TPU v7x, 32 devices: a whole 2x2x4 slice. The times are simulated.
32 devices in a mesh: section: 4 (over y, x), tp: 8 (over z, core).
Axes of the slice: x: 2, y: 2, z: 4, core: 2. Of those that a mesh axis runs over, the one named last changes fastest.
Arguments:
- grad_in: bfloat16 [4, 128, 4096], P('section', None, 'tp'), may hold values from -6 to 6
- fresh_grads: bfloat16 [1, 128, 4096], P(None, None, 'tp'), may hold values from -6 to 6
- acc_in: float32 [4, 128, 4096], P('section', None, 'tp'), may hold values from -3 to 3
- queries: bfloat16 [4, 2, 128, 4096], P('section', None, None, 'tp'), may hold values from -4.625 to 4.625
- keys: bfloat16 [4, 2, 128, 4096], P('section', None, None, 'tp'), may hold values from -4.625 to 4.625
- values: bfloat16 [4, 2, 128, 4096], P('section', None, None, 'tp'), may hold values from -12 to 12
- query_weight: bfloat16 [4, 4096, 4096], P('section', 'tp'), may hold values from -0.09375 to 0.09375
- key_weight: bfloat16 [4, 4096, 4096], P('section', None, 'tp'), may hold values from -0.125 to 0.125
- value_weight: bfloat16 [4, 4096, 4096], P('section', None, 'tp'), may hold values from -0.125 to 0.125
- out_weight: bfloat16 [4, 4096, 4096], P('section', 'tp'), may hold values from -0.09375 to 0.09375
Outputs:
- grad_out: bfloat16 [4, 128, 4096], P('section', None, 'tp')
- acc_out: float32 [4, 128, 4096], P('section', None, 'tp')
All inputs are finite; a program needn't handle non-finite values.
Results may differ from a plain program's by a relative error of at most 0.025.
Values may be sent and summed in bfloat16 or wider, within the bound.
A program may use at most 64 MiB of HBM per device.

v0:
```python
import jax
import jax.numpy as jnp
from jax import lax
from jax.sharding import PartitionSpec as P

HEAD_DIM = 64
SEQS = 1


def passed_along(value, axis, steps):
    count = lax.axis_size(axis)
    leading, last = (max(0, -steps), min(count, count - steps))
    return lax.ppermute(value, axis, [(source, source + steps) for source in range(leading, last)])


def transpose_product(left, right):
    return lax.dot_general(
        left, right, (((1,), (1,)), ((), ())), preferred_element_type=jnp.float32
    )


def attention_grads(upstream, queries, keys, values):
    token_rows, columns = queries.shape
    enc_rows = keys.shape[0]
    heads = columns // HEAD_DIM
    query_heads = queries.reshape(SEQS, token_rows // SEQS, heads, HEAD_DIM)
    key_heads = keys.reshape(SEQS, enc_rows // SEQS, heads, HEAD_DIM)
    value_heads = values.reshape(SEQS, enc_rows // SEQS, heads, HEAD_DIM)
    upstream_heads = upstream.reshape(SEQS, token_rows // SEQS, heads, HEAD_DIM)
    scores = jnp.einsum(
        "bqhd,bkhd->bhqk", query_heads, key_heads, preferred_element_type=jnp.float32
    )
    attention = jax.nn.softmax(scores, axis=-1)
    weights = attention.astype(jnp.bfloat16)
    output = jnp.einsum("bhqk,bkhd->bqhd", weights, value_heads, preferred_element_type=jnp.float32)
    delta = jnp.sum(upstream_heads.astype(jnp.float32) * output, axis=-1)
    prob_grad = jnp.einsum(
        "bqhd,bkhd->bhqk", upstream_heads, value_heads, preferred_element_type=jnp.float32
    )
    score_grad = (attention * (prob_grad - jnp.transpose(delta, (0, 2, 1))[..., None])).astype(
        jnp.bfloat16
    )
    query_grad = jnp.einsum(
        "bhqk,bkhd->bqhd", score_grad, key_heads, preferred_element_type=jnp.float32
    )
    key_grad = jnp.einsum(
        "bhqk,bqhd->bkhd", score_grad, query_heads, preferred_element_type=jnp.float32
    )
    value_grad = jnp.einsum(
        "bhqk,bqhd->bkhd", weights, upstream_heads, preferred_element_type=jnp.float32
    )
    return (
        query_grad.reshape(token_rows, columns).astype(jnp.bfloat16),
        key_grad.reshape(enc_rows, columns).astype(jnp.bfloat16),
        value_grad.reshape(enc_rows, columns).astype(jnp.bfloat16),
    )


def body(
    grad_in,
    fresh_grads,
    acc_in,
    queries,
    keys,
    values,
    query_weight,
    key_weight,
    value_weight,
    out_weight,
):
    grad_slice = grad_in[0]
    carried = acc_in[0]
    w_query = query_weight[0]
    w_key = key_weight[0]
    w_value = value_weight[0]
    w_out = out_weight[0]
    slot_count = queries.shape[1]
    is_top = lax.axis_index("section") == lax.axis_size("section") - 1
    passed = grad_slice
    for slot in range(slot_count):
        upstream = transpose_product(lax.all_gather(grad_slice, "tp", axis=1, tiled=True), w_out)
        query_grad, key_grad, value_grad = attention_grads(
            upstream.astype(jnp.bfloat16), queries[0, slot], keys[0, slot], values[0, slot]
        )
        branch = transpose_product(lax.all_gather(query_grad, "tp", axis=1, tiled=True), w_query)
        passed = (grad_slice.astype(jnp.float32) + branch).astype(jnp.bfloat16)
        passes_on = slot + 1 < slot_count
        summed = carried
        term = transpose_product(key_grad, w_key) + transpose_product(value_grad, w_value)
        summed = summed + lax.psum_scatter(
            term.astype(jnp.bfloat16), "tp", scatter_dimension=1, tiled=True
        ).astype(jnp.float32)
        if passes_on:
            summed = passed_along(summed.astype(jnp.bfloat16), "section", -1).astype(summed.dtype)
        carried = summed
        if passes_on:
            received = passed_along(passed, "section", -1)
            new_slice = jnp.where(is_top, fresh_grads[slot], received)
            grad_slice = new_slice
            pass
    return (passed[None], carried[None])


def solution(mesh):
    in_specs = (
        P("section", None, "tp"),
        P(None, None, "tp"),
        P("section", None, "tp"),
        P("section", None, None, "tp"),
        P("section", None, None, "tp"),
        P("section", None, None, "tp"),
        P("section", "tp", None),
        P("section", None, "tp"),
        P("section", None, "tp"),
        P("section", "tp", None),
    )
    out_specs = (P("section", None, "tp"), P("section", None, "tp"))
    return jax.shard_map(body, mesh=mesh, in_specs=in_specs, out_specs=out_specs, check_vma=False)
```

profile of v0, /device:TPU:0, one launch (start us, length us, event | category | flops | bytes accessed | tf_op | source)
XLA Modules:
  0.0 196.2 jit_solution(3689854424168437821)
XLA Ops:
  7.2 0.7 all-gather.12.cloned.1.call-update
  7.9 1.0 fusion.55
  8.9 0.1 copy.34
  9.1 1.0 fusion.57
  10.1 0.1 copy.35
  10.2 1.0 fusion.56
  11.2 0.1 copy.37
  11.3 0.4 fusion.58
  11.7 22.9 %all-gather.12.cloned.1.call-done = bf16[1,128,4096]{2,1,0:T(8,128)(2,1)} async-done(((bf16[1,128,512]{2,1,0:T(8,128)(2,1)}), bf16[1,128,4096]{2,1,0:T(8,128)(2,1)}) %all-gather.12.cloned.1.call-update) | async-done | bytes 1048592 | tf_op jit(solution)/shard_map/all_gather | solution.py:81
  34.6 4.0 %fusion.31 = bf16[128,512]{1,0:T(8,128)(2,1)S(1)} fusion(bf16[1,512,4096]{2,1,0:T(8,128)(2,1)} %param.19, bf16[1,128,4096]{2,1,0:T(8,128)(2,1)} %all-gather.12.cloned.1.call-done), kind=kOutput, calls=%fused_computation.35 | convolution fusion | flops 536936448 | bytes 5373952 | tf_op jit(solution)/shard_map/dot_general | solution.py:17
  38.6 0.1 copy.36
  38.7 0.1 copy.38
  38.9 0.2 fusion.40
  39.1 0.3 fusion.25
  39.4 0.9 convolution_convert_fusion.1
  40.3 21.9 %all-gather.6.cloned.1.call-done = bf16[128,4096]{0,1:T(8,128)(2,1)} async-done(((bf16[128,512]{0,1:T(8,128)(2,1)}), bf16[128,4096]{0,1:T(8,128)(2,1)}) %all-gather.6.cloned.1.call-update) | async-done | bytes 1048592 | tf_op jit(solution)/shard_map/all_gather | solution.py:85
  62.3 4.0 %fusion.37 = bf16[128,512]{1,0:T(8,128)(2,1)S(1)} fusion(bf16[128,4096]{0,1:T(8,128)(2,1)} %all-gather.6.cloned.1.call-done, bf16[1,512,4096]{2,1,0:T(8,128)(2,1)} %param.16, bf16[1,128,512]{2,1,0:T(8,128)(2,1)S(1)} %copy-done.3), kind=kOutput, calls=%fused_computation.43 | convolution fusion | flops 537067520 | bytes 5505024 | tf_op jit(solution)/shard_map/dot_general | solution.py:17
  66.3 1.3 collective-permute-start
  67.6 6.2 %collective-permute-done = bf16[128,512]{1,0:T(8,128)(2,1)S(1)} collective-permute-done((bf16[128,512]{1,0:T(8,128)(2,1)S(1)}, bf16[128,512]{1,0:T(8,128)(2,1)S(1)}, u32[]{:S(2)}, u32[]{:S(2)}) %collective-permute-start) | collective-permute-done | bytes 131104 | tf_op jit(solution)/shard_map/ppermute | solution.py:13
  73.8 0.7 bitcast_select_fusion
  74.5 0.0 reduce-scatter.3.cloned.1.call-start
  74.6 0.3 convolution_convert_fusion.5
  74.9 0.3 convolution_convert_fusion.4
  75.2 3.8 %fusion.8 = f32[128,4096]{1,0:T(8,128)S(1)} fusion(bf16[128,512]{0,1:T(8,128)(2,1)S(1)} %bitcast.159, bf16[1,4096,512]{2,1,0:T(8,128)(2,1)} %param.17), kind=kOutput, calls=%fused_computation.10 | convolution fusion | flops 536870912 | bytes 6422528 | tf_op jit(solution)/shard_map/dot_general | solution.py:17
  79.0 2.5 %fusion.2 = bf16[128,4096]{1,0:T(8,128)(2,1)} fusion(f32[128,4096]{1,0:T(8,128)S(1)} %fusion.8, bf16[128,512]{0,1:T(8,128)(2,1)S(1)} %bitcast.165, bf16[1,4096,512]{2,1,0:T(8,128)(2,1)S(1)} %copy-done), kind=kOutput, calls=%fused_computation.4 | convolution fusion | flops 537919488 | bytes 7471104 | tf_op jit(solution)/shard_map/dot_general | solution.py:17
  81.6 0.1 copy.42
  81.7 0.1 copy.43
  81.8 0.1 copy.45
  81.9 0.4 fusion.59
  82.3 14.2 %all-gather.8.cloned.1.call-done = bf16[128,4096]{1,0:T(8,128)(2,1)} async-done(((bf16[128,512]{1,0:T(8,128)(2,1)}), bf16[128,4096]{1,0:T(8,128)(2,1)}) %all-gather.8.cloned.1.call-update) | async-done | bytes 1048592 | tf_op jit(solution)/shard_map/all_gather | solution.py:81
  96.5 4.0 %fusion.34 = bf16[128,512]{1,0:T(8,128)(2,1)S(1)} fusion(bf16[128,4096]{1,0:T(8,128)(2,1)} %all-gather.8.cloned.1.call-done, bf16[1,512,4096]{2,1,0:T(8,128)(2,1)} %param.19), kind=kOutput, calls=%fused_computation.36 | convolution fusion | flops 536936448 | bytes 5373952 | tf_op jit(solution)/shard_map/dot_general | solution.py:17
  100.5 0.1 copy.44
  100.7 0.1 copy.46
  100.8 0.2 fusion.41
  101.0 0.3 fusion.24
  101.3 0.9 convolution_convert_fusion
  102.2 0.0 reduce-scatter.5.cloned.1.call-start
  102.2 0.3 convolution_convert_fusion.3
  102.5 0.3 convolution_convert_fusion.2
  102.8 3.9 %fusion.6 = f32[128,4096]{1,0:T(8,128)S(1)} fusion(bf16[128,512]{0,1:T(8,128)(2,1)S(1)} %bitcast.160, bf16[1,4096,512]{2,1,0:T(8,128)(2,1)} %param.17), kind=kOutput, calls=%fused_computation.8 | convolution fusion | flops 536870912 | bytes 6422528 | tf_op jit(solution)/shard_map/dot_general | solution.py:17
  106.8 2.5 %fusion.3 = bf16[128,4096]{1,0:T(8,128)(2,1)} fusion(f32[128,4096]{1,0:T(8,128)S(1)} %fusion.6, bf16[128,512]{0,1:T(8,128)(2,1)S(1)} %bitcast.166, bf16[1,4096,512]{2,1,0:T(8,128)(2,1)S(1)} %copy-done.1), kind=kOutput, calls=%fused_computation.5 | convolution fusion | flops 537919488 | bytes 7471104 | tf_op jit(solution)/shard_map/dot_general | solution.py:17
  109.3 21.6 %reduce-scatter.3.cloned.1.call-done = bf16[128,512]{1,0:T(8,128)(2,1)} async-done(((bf16[128,4096]{1,0:T(8,128)(2,1)}), bf16[128,512]{1,0:T(8,128)(2,1)}) %reduce-scatter.3.cloned.1.call-update) | async-done | bytes 131088 | tf_op jit(solution)/shard_map/reduce_scatter | solution.py:90
  130.9 0.9 fusion.43
  131.8 1.3 collective-permute-start.1
  133.1 20.2 %all-gather.10.cloned.1.call-done = bf16[128,4096]{0,1:T(8,128)(2,1)} async-done(((bf16[128,512]{0,1:T(8,128)(2,1)}), bf16[128,4096]{0,1:T(8,128)(2,1)}) %all-gather.10.cloned.1.call-update) | async-done | bytes 1048592 | tf_op jit(solution)/shard_map/all_gather | solution.py:85
  153.4 4.7 %fusion.46 = bf16[1,128,512]{2,1,0:T(8,128)(2,1)} fusion(bf16[128,512]{1,0:T(8,128)(2,1)S(1)} %copy-done.2, bf16[128,4096]{0,1:T(8,128)(2,1)} %all-gather.10.cloned.1.call-done, bf16[1,512,4096]{2,1,0:T(8,128)(2,1)} %param.16), kind=kOutput, calls=%fused_computation.55 | convolution fusion | flops 537067520 | bytes 5505024 | tf_op jit(solution)/shard_map/dot_general | solution.py:17
  158.1 29.6 %reduce-scatter.5.cloned.1.call-done = bf16[128,512]{1,0:T(8,128)(2,1)} async-done(((bf16[128,4096]{1,0:T(8,128)(2,1)}), bf16[128,512]{1,0:T(8,128)(2,1)}) %reduce-scatter.5.cloned.1.call-update) | async-done | bytes 131088 | tf_op jit(solution)/shard_map/reduce_scatter | solution.py:90
  187.7 1.6 add_bitcast_fusion
  (22 shorter events, 0.3 us)
Async XLA Ops:
  7.2 27.4 %all-gather.12.cloned.1.call-start = ((), (), s32[]{:S(2)}) async-start(), calls=%async_computation.7 | async-start | bytes 1179648 | tf_op jit(solution)/shard_map/all_gather | solution.py:81
  7.9 54.4 %all-gather.6.cloned.1.call-start = ((), (), s32[]{:S(2)}) async-start(), calls=%async_computation.2 | async-start | bytes 1179648 | tf_op jit(solution)/shard_map/all_gather | solution.py:85
  11.7 50.6 %copy-start.3 = (bf16[1,128,512]{2,1,0:T(8,128)(2,1)S(1)}, bf16[1,128,512]{2,1,0:T(8,128)(2,1)}, u32[]{:S(2)}) copy-start(bf16[1,128,512]{2,1,0:T(8,128)(2,1)} %param.10) | copy-start | bytes 393220
  39.1 34.8 %copy-start.5 = (bf16[1,128,512]{2,1,0:T(8,128)(2,1)S(1)}, bf16[1,128,512]{2,1,0:T(8,128)(2,1)}, u32[]{:S(2)}) copy-start(bf16[1,128,512]{2,1,0:T(8,128)(2,1)} %param.11) | copy-start | bytes 393220
  40.3 56.2 %all-gather.8.cloned.1.call-start = ((), (), s32[]{:S(2)}) async-start(), calls=%async_computation.3 | async-start | bytes 1179648 | tf_op jit(solution)/shard_map/all_gather | solution.py:81
  66.3 7.5 %collective-permute-start = (bf16[128,512]{1,0:T(8,128)(2,1)S(1)}, bf16[128,512]{1,0:T(8,128)(2,1)S(1)}, u32[]{:S(2)}, u32[]{:S(2)}) collective-permute-start(bf16[128,512]{1,0:T(8,128)(2,1)S(1)} %fusion.37), channel_id=1, source_target_pairs={{8,0},{16,8},{24,16},{9,1},{17,9},{25,17},{10,2},{18,10},{26,18},{... | collective-permute-start | bytes 393224 | tf_op jit(solution)/shard_map/ppermute | solution.py:13
  74.5 56.4 %reduce-scatter.3.cloned.1.call-start = ((), (), s32[]{:S(2)}) async-start(), calls=%async_computation.5 | async-start | bytes 1179648 | tf_op jit(solution)/shard_map/reduce_scatter | solution.py:90
  74.9 4.2 %copy-start = (bf16[1,4096,512]{2,1,0:T(8,128)(2,1)S(1)}, bf16[1,4096,512]{2,1,0:T(8,128)(2,1)}, u32[]{:S(2)}) copy-start(bf16[1,4096,512]{2,1,0:T(8,128)(2,1)} %param.18) | copy-start | bytes 12582916
  81.5 71.9 %all-gather.10.cloned.1.call-start = ((), (), s32[]{:S(2)}) async-start(), calls=%async_computation.4 | async-start | bytes 1179648 | tf_op jit(solution)/shard_map/all_gather | solution.py:85
  102.2 85.5 %reduce-scatter.5.cloned.1.call-start = ((), (), s32[]{:S(2)}) async-start(), calls=%async_computation.6 | async-start | bytes 1179648 | tf_op jit(solution)/shard_map/reduce_scatter | solution.py:90
  102.5 4.3 %copy-start.1 = (bf16[1,4096,512]{2,1,0:T(8,128)(2,1)S(1)}, bf16[1,4096,512]{2,1,0:T(8,128)(2,1)}, u32[]{:S(2)}) copy-start(bf16[1,4096,512]{2,1,0:T(8,128)(2,1)} %param.18) | copy-start | bytes 12582916
  106.8 24.1 %copy-start.4 = (f32[1,128,512]{2,1,0:T(8,128)S(1)}, f32[1,128,512]{2,1,0:T(8,128)}, u32[]{:S(2)}) copy-start(f32[1,128,512]{2,1,0:T(8,128)} %param.12) | copy-start | bytes 786436
  106.8 46.6 %copy-start.2 = (bf16[128,512]{1,0:T(8,128)(2,1)S(1)}, bf16[128,512]{1,0:T(8,128)(2,1)}, u32[]{:S(2)}) copy-start(bf16[128,512]{1,0:T(8,128)(2,1)} %bitcast_select_fusion) | copy-start | bytes 393220
  131.8 26.2 %collective-permute-start.1 = (bf16[128,512]{1,0:T(8,128)(2,1)S(1)}, bf16[128,512]{1,0:T(8,128)(2,1)S(1)}, u32[]{:S(2)}, u32[]{:S(2)}) collective-permute-start(bf16[128,512]{1,0:T(8,128)(2,1)S(1)} %fusion.43), channel_id=1, source_target_pairs={{8,0},{16,8},{24,16},{9,1},{17,9},{25,17},{10,2},{18,10},{26,18},{... | collective-permute-start | bytes 393224 | tf_op jit(solution)/shard_map/ppermute | solution.py:13
Sparse Core Ops, SparseCore 0:
  9.6 24.9 all-gather.11
  40.4 21.8 all-gather.5
  74.7 21.7 all-gather.7
  98.6 32.2 reduce-scatter.2
  132.9 20.4 all-gather.9
  155.5 32.1 reduce-scatter.4
where the time goes:
time: 196 us
  waiting for transfers between devices  137 us (70%)
  matrix products  34.1 us (17%)
  between operations  14.3 us (7%)
  local copies, waits for them, and re-layouts  4.18 us (2%)
  other arithmetic  3.24 us (2%)
  starting transfers between devices  2.83 us (1%)
    reduce_scatter x2, waiting for transfers between devices, body(): lax.psum_scatter(term.astype(jnp.bfloat16), 'tp', scatter_dimension=1, ti...  51.2 us
    all_gather x2, waiting for transfers between devices, body(): lax.all_gather(query_grad, 'tp', axis=1, tiled=True)  42.2 us
    all_gather x2, waiting for transfers between devices, body(): lax.all_gather(grad_slice, 'tp', axis=1, tiled=True)  37.1 us
    dot_general x8, matrix products, transpose_product(): lax.dot_general(left, right, (((1,), (1,)), ((), ())), preferred_element_...  29.5 us
    ppermute x2, waiting for transfers between devices, passed_along(): lax.ppermute(value, axis, [(source, source + steps) for source in range(l...  6.21 us
  transfers between devices with their start and end apart: 8, of which 7 were waited for; matrix products, arithmetic and copies ran while one was open for 15% of the time, Pallas kernels for 0%

commit v1 on v0

v1 whole, which is shorter than its diff:
```python
import functools

import jax
import jax.numpy as jnp
from jax import lax
from jax.experimental import pallas as pl
from jax.experimental.pallas import tpu as pltpu
from jax.sharding import PartitionSpec as P

HEAD_DIM = 64
LANES = 128
CHUNKS = 2
MESH = pl.DeviceIdType.MESH
F32, BF16 = jnp.float32, jnp.bfloat16


def nt(left, right):
    return lax.dot_general(left, right, (((1,), (1,)), ((), ())), preferred_element_type=F32)


def tn(left, right):
    return lax.dot_general(left, right, (((0,), (0,)), ((), ())), preferred_element_type=F32)


def nn(left, right):
    return lax.dot_general(left, right, (((1,), (0,)), ((), ())), preferred_element_type=F32)


def kernel(
    n_sections, n_tp, slots,
    grad_in, fresh, acc_in, queries, keys, values, wq_hbm, wk_hbm, wv_hbm, wo_hbm,
    grad_out, acc_out,
    wq, wk, wv, wo, gbuf, gathered, qgrad, kgrad, vgrad, total, passed_buf,
    own_term, part_out, part_in, right_out, right_in, left_out, left_in, acc_send, acc_recv,
    load_sem, ag_send, ag_recv, part_sem, right_sem, left_sem, pass_sem, acc_sem,
):
    section = lax.axis_index("section")
    me = lax.axis_index("tp")
    chips = n_tp // 2
    chip, core = me // 2, me % 2
    other = 1 - core
    partner = chip * 2 + other
    rows, width = grad_in.shape[1], grad_in.shape[2]
    columns = queries.shape[3]
    piece = rows // CHUNKS
    has_left, has_right = chip > 0, chip < chips - 1
    top = section == n_sections - 1

    def load(source, target, n):
        return pltpu.make_async_copy(source, target, load_sem.at[n])

    loads = [
        load(grad_in.at[0], gbuf.at[0], 0),
        load(wo_hbm.at[0], wo, 1),
        load(wk_hbm.at[0], wk, 2),
        load(wv_hbm.at[0], wv, 3),
        load(wq_hbm.at[0], wq, 4),
    ]
    for one in loads:
        one.start()

    barrier = pltpu.get_barrier_semaphore()

    def greet(condition, device):
        @pl.when(condition)
        def _():
            pl.semaphore_signal(barrier, inc=1, device_id=device, device_id_type=MESH)

    neighbours = [
        (core >= 0, {"tp": partner}),
        (has_left, {"tp": me - 2}),
        (has_right, {"tp": me + 2}),
        (section > 0, {"section": section - 1}),
        (section < n_sections - 1, {"section": section + 1}),
    ]
    for condition, device in neighbours:
        greet(condition, device)
    pl.semaphore_wait(barrier, sum(jnp.where(condition, 1, 0) for condition, _ in neighbours))

    def part_of(c):
        return pl.ds(c * piece, piece)

    def block_copy(source, i, block, c, way, device):
        return pltpu.make_async_remote_copy(
            src_ref=source.at[part_of(c)],
            dst_ref=gathered.at[i, block, part_of(c)],
            send_sem=ag_send.at[i, block // 2, c, way],
            recv_sem=ag_recv.at[i, block, c],
            device_id={"tp": device},
            device_id_type=MESH,
        )

    def start_gather(i, source):
        for c in range(CHUNKS):
            @pl.when(has_right)
            def _():
                block_copy(source, i, me, c, 0, me + 2).start()

            @pl.when(has_left)
            def _():
                block_copy(source, i, me, c, 1, me - 2).start()

        for c in range(CHUNKS):
            block_copy(source, i, me, c, 2, partner).start()

    def relay(i, h):
        for c in range(CHUNKS):
            @pl.when((h > 0) & (chip - h >= 0))
            def _():
                block = (chip - h) * 2 + core
                held = gathered.at[i, block]
                block_copy(held, i, block, c, 2, partner).wait_recv()

                @pl.when(has_right)
                def _():
                    block_copy(held, i, block, c, 0, me + 2).start()

                block_copy(held, i, block, c, 2, partner).start()

            @pl.when((h > 0) & (chip + h < chips))
            def _():
                block = (chip + h) * 2 + core
                held = gathered.at[i, block]
                block_copy(held, i, block, c, 2, partner).wait_recv()

                @pl.when(has_left)
                def _():
                    block_copy(held, i, block, c, 1, me - 2).start()

                block_copy(held, i, block, c, 2, partner).start()

    def add_block(i, weight, block):
        at = pl.ds(pl.multiple_of(block * (weight.shape[1] // n_tp), LANES), weight.shape[1] // n_tp)
        total[...] += nt(gathered[i, block], weight[:, at])

    def take(i, weight, h):
        for condition, chip_of in (((h > 0) & (chip - h >= 0), chip - h), ((h > 0) & (chip + h < chips), chip + h)):
            @pl.when(condition)
            def _():
                add_block(i, weight, chip_of * 2 + core)

    def take_partner(i, weight, h):
        for condition, chip_of in (((h >= 0) & (chip - h >= 0), chip - h), ((h > 0) & (chip + h < chips), chip + h)):
            @pl.when(condition)
            def _():
                block = chip_of * 2 + other
                for c in range(CHUNKS):
                    block_copy(gathered.at[i, block], i, block, c, 2, partner).wait_recv()
                add_block(i, weight, block)

    def own_block(source, weight):
        at = pl.ds(pl.multiple_of(me * (weight.shape[1] // n_tp), LANES), weight.shape[1] // n_tp)
        total[...] = nt(source[...], weight[:, at])

    def wait_gather_sends(i, source):
        @pl.loop(0, chips)
        def _(o):
            block = o * 2 + core
            for c in range(CHUNKS):
                @pl.when(has_right & (o <= chip))
                def _():
                    block_copy(source, i, block, c, 0, me + 2).wait_send()

                @pl.when(has_left & (o >= chip))
                def _():
                    block_copy(source, i, block, c, 1, me - 2).wait_send()

                block_copy(source, i, block, c, 2, partner).wait_send()

    def attention_grads(slot):
        lane = lax.broadcasted_iota(jnp.int32, (1, LANES), 1)
        masks = [
            ((lane >= n * HEAD_DIM) & (lane < (n + 1) * HEAD_DIM)).astype(F32).astype(BF16)
            for n in range(LANES // HEAD_DIM)
        ]
        for pair in range(columns // LANES):
            at = pl.ds(pair * LANES, LANES)
            query, key, value = queries[0, slot, :, at], keys[0, slot, :, at], values[0, slot, :, at]
            upstream = total[:, at].astype(BF16)
            dq, dk, dv = 0.0, 0.0, 0.0
            for mask in masks:
                key_h = key * mask
                scores = nt(query, key_h)
                prob_grad = nt(upstream, value * mask)
                shifted = jnp.exp(scores - jnp.max(scores, axis=1, keepdims=True))
                attention = shifted / jnp.sum(shifted, axis=1, keepdims=True)
                weights = attention.astype(BF16)
                delta = jnp.sum(weights.astype(F32) * prob_grad, axis=1, keepdims=True)
                score_grad = (attention * (prob_grad - delta)).astype(BF16)
                dq = dq + nn(score_grad, key_h)
                dk = dk + tn(score_grad, query * mask)
                dv = dv + tn(weights, upstream * mask)
            qgrad[slot, :, at] = dq.astype(BF16)
            kgrad[:, at] = dk.astype(BF16)
            vgrad[:, at] = dv.astype(BF16)

    def part_copy(slot, z):
        return pltpu.make_async_remote_copy(
            src_ref=part_out.at[slot, z], dst_ref=part_in.at[slot, z],
            send_sem=part_sem.at[0, slot, z], recv_sem=part_sem.at[1, slot, z],
            device_id={"tp": partner}, device_id_type=MESH,
        )

    def right_copy(slot, z):
        return pltpu.make_async_remote_copy(
            src_ref=right_out.at[slot, z], dst_ref=right_in.at[slot, z],
            send_sem=right_sem.at[0, slot, z], recv_sem=right_sem.at[1, slot, z],
            device_id={"tp": me + 2}, device_id_type=MESH,
        )

    def left_copy(slot, z):
        return pltpu.make_async_remote_copy(
            src_ref=left_out.at[slot, z], dst_ref=left_in.at[slot, z],
            send_sem=left_sem.at[0, slot, z], recv_sem=left_sem.at[1, slot, z],
            device_id={"tp": me - 2}, device_id_type=MESH,
        )

    def term_block(z, core_of):
        at = pl.ds(pl.multiple_of((z * 2 + core_of) * width, LANES), width)
        return nt(kgrad[...], wk[at, :]) + nt(vgrad[...], wv[at, :])

    def make_terms(slot):
        @pl.loop(0, chips)
        def _(z):
            part_out[slot, z] = term_block(z, other).astype(BF16)
            part_copy(slot, z).start()

        @pl.loop(0, chips)
        def _(z):
            own_term[z] = term_block(z, core)

    def sum_step(slot, h):
        @pl.when(chip == h)
        def _():
            @pl.loop(0, chips)
            def _(j):
                z = chips - 1 - j

                @pl.when(z > chip)
                def _():
                    part_copy(slot, z).wait_recv()

                    @pl.when(has_left)
                    def _():
                        right_copy(slot, z).wait_recv()
                        own_term[z] += right_in[slot, z].astype(F32)

                    right_out[slot, z] = (own_term[z] + part_in[slot, z].astype(F32)).astype(BF16)
                    right_copy(slot, z).start()

        @pl.when(chips - 1 - chip == h)
        def _():
            @pl.loop(0, chips)
            def _(z):
                @pl.when(z < chip)
                def _():
                    part_copy(slot, z).wait_recv()

                    @pl.when(has_right)
                    def _():
                        left_copy(slot, z).wait_recv()
                        own_term[z] += left_in[slot, z].astype(F32)

                    left_out[slot, z] = (own_term[z] + part_in[slot, z].astype(F32)).astype(BF16)
                    left_copy(slot, z).start()

    def finish_sum(slot):
        part_copy(slot, chip).wait_recv()
        own_term[chip] += part_in[slot, chip].astype(F32)

        @pl.when(has_left)
        def _():
            right_copy(slot, chip).wait_recv()
            own_term[chip] += right_in[slot, chip].astype(F32)

        @pl.when(has_right)
        def _():
            left_copy(slot, chip).wait_recv()
            own_term[chip] += left_in[slot, chip].astype(F32)

        @pl.when(slot == 0)
        def _():
            own_term[chip] += acc_in[0]

        @pl.when((slot > 0) & (section < n_sections - 1))
        def _():
            acc_copy(slot).wait_recv()
            own_term[chip] += acc_recv[slot].astype(F32)

        @pl.when(slot == slots - 1)
        def _():
            acc_out[0] = own_term[chip]

        @pl.when((slot < slots - 1) & (section > 0))
        def _():
            acc_send[slot] = own_term[chip].astype(BF16)
            acc_copy(slot + 1).start()

    def acc_copy(slot):
        return pltpu.make_async_remote_copy(
            src_ref=acc_send.at[slot - 1], dst_ref=acc_recv.at[slot],
            send_sem=acc_sem.at[0, slot], recv_sem=acc_sem.at[1, slot],
            device_id={"section": section - 1}, device_id_type=MESH,
        )

    def pass_copy(slot):
        return pltpu.make_async_remote_copy(
            src_ref=passed_buf.at[slot - 1], dst_ref=gbuf.at[slot],
            send_sem=pass_sem.at[0, slot], recv_sem=pass_sem.at[1, slot],
            device_id={"section": section - 1}, device_id_type=MESH,
        )

    def fresh_copy(slot):
        return pltpu.make_async_copy(fresh.at[slot - 1], gbuf.at[slot], pass_sem.at[1, slot])

    @pl.loop(0, slots)
    def _(slot):
        @pl.when(slot == 0)
        def _():
            loads[0].wait()

        @pl.when((slot > 0) & top)
        def _():
            fresh_copy(slot).start()
            fresh_copy(slot).wait()

        @pl.when((slot > 0) & (section < n_sections - 1))
        def _():
            pass_copy(slot).wait_recv()

        first = slot * 2
        second = first + 1
        start_gather(first, gbuf.at[slot])

        @pl.when(slot == 0)
        def _():
            loads[1].wait()

        own_block(gbuf.at[slot], wo)

        @pl.loop(1, chips)
        def _(h):
            relay(first, h)
            take(first, wo, h)
            take_partner(first, wo, h - 1)

        take_partner(first, wo, chips - 1)
        attention_grads(slot)
        start_gather(second, qgrad.at[slot])

        @pl.when(slot == 0)
        def _():
            loads[2].wait()
            loads[3].wait()

        make_terms(slot)

        @pl.when(slot == 0)
        def _():
            loads[4].wait()

        own_block(qgrad.at[slot], wq)

        @pl.loop(0, chips)
        def _(h):
            relay(second, h)
            sum_step(slot, h)
            take(second, wq, h)
            take_partner(second, wq, h - 1)

        take_partner(second, wq, chips - 1)
        result = (gbuf[slot].astype(F32) + total[...]).astype(BF16)

        @pl.when(slot == slots - 1)
        def _():
            grad_out[0] = result

        @pl.when((slot < slots - 1) & (section > 0))
        def _():
            passed_buf[slot] = result
            pass_copy(slot + 1).start()

        finish_sum(slot)

    @pl.loop(0, slots)
    def _(slot):
        wait_gather_sends(slot * 2, gbuf.at[slot])
        wait_gather_sends(slot * 2 + 1, qgrad.at[slot])

        @pl.loop(0, chips)
        def _(z):
            part_copy(slot, z).wait_send()

            @pl.when((z > chip) & has_right)
            def _():
                right_copy(slot, z).wait_send()

            @pl.when((z < chip) & has_left)
            def _():
                left_copy(slot, z).wait_send()

        @pl.when((slot > 0) & (section > 0))
        def _():
            pass_copy(slot).wait_send()
            acc_copy(slot).wait_send()


def solution(mesh):
    n_sections, n_tp = mesh.shape["section"], mesh.shape["tp"]

    def body(grad_in, fresh, acc_in, queries, keys, values, wq, wk, wv, wo):
        slots = queries.shape[1]
        rows, width = grad_in.shape[1:]
        columns = queries.shape[3]
        chips = n_tp // 2
        vmem = pl.BlockSpec(memory_space=pltpu.VMEM)
        hbm = pl.BlockSpec(memory_space=pl.ANY)
        block = (slots, chips, rows, width)
        scratch = [
            pltpu.VMEM(wq.shape[1:], BF16),
            pltpu.VMEM(wk.shape[1:], BF16),
            pltpu.VMEM(wv.shape[1:], BF16),
            pltpu.VMEM(wo.shape[1:], BF16),
            pltpu.VMEM((slots, rows, width), BF16),
            pltpu.VMEM((2 * slots, n_tp, rows, width), BF16),
            pltpu.VMEM((slots, rows, columns), BF16),
            pltpu.VMEM((rows, columns), BF16),
            pltpu.VMEM((rows, columns), BF16),
            pltpu.VMEM((rows, columns), F32),
            pltpu.VMEM((slots, rows, width), BF16),
            pltpu.VMEM((chips, rows, width), F32),
        ]
        scratch += [pltpu.VMEM(block, BF16)] * 6
        scratch += [pltpu.VMEM((slots, rows, width), BF16)] * 2
        dma = pltpu.SemaphoreType.DMA
        scratch += [
            dma((5,)),
            dma((2 * slots, chips, CHUNKS, 3)),
            dma((2 * slots, n_tp, CHUNKS)),
            dma((2, slots, chips)),
            dma((2, slots, chips)),
            dma((2, slots, chips)),
            dma((2, slots)),
            dma((2, slots)),
        ]
        return pl.pallas_call(
            functools.partial(kernel, n_sections, n_tp, slots),
            out_shape=(
                jax.ShapeDtypeStruct(grad_in.shape, BF16),
                jax.ShapeDtypeStruct(acc_in.shape, F32),
            ),
            in_specs=[hbm, hbm, vmem, vmem, vmem, vmem, hbm, hbm, hbm, hbm],
            out_specs=(vmem, vmem),
            scratch_shapes=scratch,
            compiler_params=pltpu.CompilerParams(
                collective_id=0, has_side_effects=True, vmem_limit_bytes=60 * 1024 * 1024
            ),
        )(grad_in, fresh, acc_in, queries, keys, values, wq, wk, wv, wo)

    in_specs = (
        P("section", None, "tp"),
        P(None, None, "tp"),
        P("section", None, "tp"),
        P("section", None, None, "tp"),
        P("section", None, None, "tp"),
        P("section", None, None, "tp"),
        P("section", "tp", None),
        P("section", None, "tp"),
        P("section", None, "tp"),
        P("section", "tp", None),
    )
    out_specs = (P("section", None, "tp"), P("section", None, "tp"))
    return jax.shard_map(body, mesh=mesh, in_specs=in_specs, out_specs=out_specs, check_vma=False)
```

time: 196 us -> 87.8 us (0.45)
  waiting for transfers between devices: 137 us -> 0 us
  Pallas kernels: 0 us -> 83.8 us
  matrix products: 34.1 us -> 0 us
  between operations: 14.3 us -> 0.64 us
  other arithmetic: 3.24 us -> 0 us
  starting transfers between devices: 2.83 us -> 0 us
    pallas_call x0 -> x1, Pallas kernels: none -> 83.8 us  [body(): pl.pallas_call(functools.partial(kernel, n_sections, n_tp, slots), out_sh...]
    all_gather x4 -> x0, waiting for transfers between devices: 79.3 us -> none  [the longest x2 42.2 us: body(): lax.all_gather(query_grad, 'tp', axis=1, tiled=True)]
    reduce_scatter x2 -> x0, waiting for transfers between devices: 51.2 us -> none  [body(): lax.psum_scatter(term.astype(jnp.bfloat16), 'tp', scatter_dimension=1, ti...]
    dot_general x18 -> x0, matrix products: 33.4 us -> none  [the longest x8 29.5 us: transpose_product(): lax.dot_general(left, right, (((1,), (1,)), ((), ())), preferred_element_...]
    ppermute x2 -> x0, waiting for transfers between devices: 6.21 us -> none  [passed_along(): lax.ppermute(value, axis, [(source, source + steps) for source in range(l...]
    slice x9 -> x0, local copies, waits for them, and re-layouts: 3.68 us -> none  [the longest x3 1.23 us: body(): values[0, slot]]
    unnamed x12 -> x2, local copies, waits for them, and re-layouts: 0.06 us -> 3.24 us
    ppermute x2 -> x0, starting transfers between devices: 2.58 us -> none  [passed_along(): lax.ppermute(value, axis, [(source, source + steps) for source in range(l...]
  transfers between devices with their start and end apart: 8 -> 0, of which waited for: 7 -> 0; matrix products, arithmetic and copies ran while one was open for 15% -> 0% of each run, Pallas kernels for 0% -> 0%
where the time goes in v1:
time: 87.8 us; the launch traced here: 87.6 us
  Pallas kernels  83.8 us (95%)
  local copies, waits for them, and re-layouts  3.24 us (4%)
    pallas_call x1, Pallas kernels, body(): pl.pallas_call(functools.partial(kernel, n_sections, n_tp, slots), out_sh...  83.8 us
    unnamed x2, local copies, waits for them, and re-layouts  3.24 us

profile of v1, /device:TPU:0, one launch (start us, length us, event | category | flops | bytes accessed | tf_op | source)
XLA Modules:
  0.0 87.6 jit_solution(8627716348681255672)
XLA Ops:
  0.6 83.8 %shard_map.113 = (bf16[1,128,512]{2,1,0:T(8,128)(2,1)}, f32[1,128,512]{2,1,0:T(8,128)}) custom-call(bf16[1,128,512]{2,1,0:T(8,128)(2,1)} %grad_in.1, bf16[1,128,512]{2,1,0:T(8,128)(2,1)} %fresh.1, f32[1,128,512]{2,1,0:T(8,128)} %acc_in.1, bf16[1,2,128,512]{3,2,1,0:T(8,128)(2,1)} %queries.1, bf16[1,2,128,512]{3,2,1,0:T(8,128)(2,1)} %keys.1, ...), custom_call_target="tpu_custom_call" | custom-call | tf_op jit(solution)/shard_map/pallas_call | solution.py:446
  84.4 1.6 %copy.14 = bf16[1,128,512]{2,1,0:T(8,128)(2,1)} copy(bf16[1,128,512]{2,1,0:T(8,128)(2,1)} %get-tuple-element.4) | data formatting | bytes 262144
  86.0 1.7 %copy.15 = f32[1,128,512]{2,1,0:T(8,128)} copy(f32[1,128,512]{2,1,0:T(8,128)} %get-tuple-element.5) | data formatting | bytes 524288

commit v2 on v1

--- a/solution.py
+++ b/solution.py
@@ -42,21 +42,24 @@
     partner = chip * 2 + other
     rows, width = grad_in.shape[1], grad_in.shape[2]
     columns = queries.shape[3]
-    piece = rows // CHUNKS
+    chunks, piece = gbuf.shape[1], gbuf.shape[3]
     has_left, has_right = chip > 0, chip < chips - 1
     top = section == n_sections - 1
 
+    def part_of(c):
+        return pl.ds(c * piece, piece)
+
     def load(source, target, n):
         return pltpu.make_async_copy(source, target, load_sem.at[n])
 
     loads = [
-        load(grad_in.at[0], gbuf.at[0], 0),
-        load(wo_hbm.at[0], wo, 1),
-        load(wk_hbm.at[0], wk, 2),
-        load(wv_hbm.at[0], wv, 3),
-        load(wq_hbm.at[0], wq, 4),
+        load(wo_hbm.at[0], wo, 0),
+        load(wk_hbm.at[0], wk, 1),
+        load(wv_hbm.at[0], wv, 2),
+        load(wq_hbm.at[0], wq, 3),
     ]
-    for one in loads:
+    first_grads = [load(grad_in.at[0, :, part_of(c)], gbuf.at[0, c], 4 + c) for c in range(chunks)]
+    for one in first_grads + loads:
         one.start()
 
     barrier = pltpu.get_barrier_semaphore()
@@ -77,34 +80,29 @@
         greet(condition, device)
     pl.semaphore_wait(barrier, sum(jnp.where(condition, 1, 0) for condition, _ in neighbours))
 
-    def part_of(c):
-        return pl.ds(c * piece, piece)
-
     def block_copy(source, i, block, c, way, device):
         return pltpu.make_async_remote_copy(
-            src_ref=source.at[part_of(c)],
-            dst_ref=gathered.at[i, block, part_of(c)],
+            src_ref=source.at[c],
+            dst_ref=gathered.at[i, block, c],
             send_sem=ag_send.at[i, block // 2, c, way],
             recv_sem=ag_recv.at[i, block, c],
             device_id={"tp": device},
             device_id_type=MESH,
         )
 
-    def start_gather(i, source):
-        for c in range(CHUNKS):
-            @pl.when(has_right)
-            def _():
-                block_copy(source, i, me, c, 0, me + 2).start()
-
-            @pl.when(has_left)
-            def _():
-                block_copy(source, i, me, c, 1, me - 2).start()
-
-        for c in range(CHUNKS):
-            block_copy(source, i, me, c, 2, partner).start()
+    def start_gather(i, source, c):
+        @pl.when(has_right)
+        def _():
+            block_copy(source, i, me, c, 0, me + 2).start()
+
+        @pl.when(has_left)
+        def _():
+            block_copy(source, i, me, c, 1, me - 2).start()
+
+        block_copy(source, i, me, c, 2, partner).start()
 
     def relay(i, h):
-        for c in range(CHUNKS):
+        for c in range(chunks):
             @pl.when((h > 0) & (chip - h >= 0))
             def _():
                 block = (chip - h) * 2 + core
@@ -129,9 +127,15 @@
 
                 block_copy(held, i, block, c, 2, partner).start()
 
+    def product(source, weight, block):
+        result = 0.0
+        for c in range(chunks):
+            at = pl.ds(pl.multiple_of(block * width + c * piece, piece), piece)
+            result = result + nt(source[c], weight[:, at])
+        return result
+
     def add_block(i, weight, block):
-        at = pl.ds(pl.multiple_of(block * (weight.shape[1] // n_tp), LANES), weight.shape[1] // n_tp)
-        total[...] += nt(gathered[i, block], weight[:, at])
+        total[...] += product(gathered.at[i, block], weight, block)
 
     def take(i, weight, h):
         for condition, chip_of in (((h > 0) & (chip - h >= 0), chip - h), ((h > 0) & (chip + h < chips), chip + h)):
@@ -144,19 +148,18 @@
             @pl.when(condition)
             def _():
                 block = chip_of * 2 + other
-                for c in range(CHUNKS):
+                for c in range(chunks):
                     block_copy(gathered.at[i, block], i, block, c, 2, partner).wait_recv()
                 add_block(i, weight, block)
 
     def own_block(source, weight):
-        at = pl.ds(pl.multiple_of(me * (weight.shape[1] // n_tp), LANES), weight.shape[1] // n_tp)
-        total[...] = nt(source[...], weight[:, at])
+        total[...] = product(source, weight, me)
 
     def wait_gather_sends(i, source):
         @pl.loop(0, chips)
         def _(o):
             block = o * 2 + core
-            for c in range(CHUNKS):
+            for c in range(chunks):
                 @pl.when(has_right & (o <= chip))
                 def _():
                     block_copy(source, i, block, c, 0, me + 2).wait_send()
@@ -167,7 +170,8 @@
 
                 block_copy(source, i, block, c, 2, partner).wait_send()
 
-    def attention_grads(slot):
+    def attention_grads(slot, then):
+        per_chunk = piece // LANES
         lane = lax.broadcasted_iota(jnp.int32, (1, LANES), 1)
         masks = [
             ((lane >= n * HEAD_DIM) & (lane < (n + 1) * HEAD_DIM)).astype(F32).astype(BF16)
@@ -190,9 +194,12 @@
                 dq = dq + nn(score_grad, key_h)
                 dk = dk + tn(score_grad, query * mask)
                 dv = dv + tn(weights, upstream * mask)
-            qgrad[slot, :, at] = dq.astype(BF16)
+            c, place = divmod(pair, per_chunk)
+            qgrad[slot, c, :, pl.ds(place * LANES, LANES)] = dq.astype(BF16)
             kgrad[:, at] = dk.astype(BF16)
             vgrad[:, at] = dv.astype(BF16)
+            if place == per_chunk - 1:
+                then(c)
 
     def part_copy(slot, z):
         return pltpu.make_async_remote_copy(
@@ -221,7 +228,8 @@
 
     def make_terms(slot):
         @pl.loop(0, chips)
-        def _(z):
+        def _(k):
+            z = (2 * chips - 1 - chip + k) % chips
             part_out[slot, z] = term_block(z, other).astype(BF16)
             part_copy(slot, z).start()
 
@@ -303,40 +311,45 @@
             device_id={"section": section - 1}, device_id_type=MESH,
         )
 
-    def pass_copy(slot):
-        return pltpu.make_async_remote_copy(
-            src_ref=passed_buf.at[slot - 1], dst_ref=gbuf.at[slot],
-            send_sem=pass_sem.at[0, slot], recv_sem=pass_sem.at[1, slot],
+    def pass_copy(slot, c):
+        return pltpu.make_async_remote_copy(
+            src_ref=passed_buf.at[slot - 1, c], dst_ref=gbuf.at[slot, c],
+            send_sem=pass_sem.at[0, slot, c], recv_sem=pass_sem.at[1, slot, c],
             device_id={"section": section - 1}, device_id_type=MESH,
         )
 
-    def fresh_copy(slot):
-        return pltpu.make_async_copy(fresh.at[slot - 1], gbuf.at[slot], pass_sem.at[1, slot])
+    def fresh_copy(slot, c):
+        return load(fresh.at[slot - 1, :, part_of(c)], gbuf.at[slot, c], 4 + c)
 
     @pl.loop(0, slots)
     def _(slot):
-        @pl.when(slot == 0)
-        def _():
-            loads[0].wait()
-
-        @pl.when((slot > 0) & top)
-        def _():
-            fresh_copy(slot).start()
-            fresh_copy(slot).wait()
-
-        @pl.when((slot > 0) & (section < n_sections - 1))
-        def _():
-            pass_copy(slot).wait_recv()
-
         first = slot * 2
         second = first + 1
-        start_gather(first, gbuf.at[slot])
+        for c in range(chunks):
+            @pl.when(slot == 0)
+            def _():
+                first_grads[c].wait()
+
+            @pl.when((slot > 0) & top)
+            def _():
+                fresh_copy(slot, c).start()
+                fresh_copy(slot, c).wait()
+
+            @pl.when((slot > 0) & (section < n_sections - 1))
+            def _():
+                pass_copy(slot, c).wait_recv()
+
+            start_gather(first, gbuf.at[slot], c)
 
         @pl.when(slot == 0)
         def _():
-            loads[1].wait()
+            loads[0].wait()
 
         own_block(gbuf.at[slot], wo)
+
+        @pl.when(slot > 0)
+        def _():
+            finish_sum(slot - 1)
 
         @pl.loop(1, chips)
         def _(h):
@@ -345,19 +358,18 @@
             take_partner(first, wo, h - 1)
 
         take_partner(first, wo, chips - 1)
-        attention_grads(slot)
-        start_gather(second, qgrad.at[slot])
+        attention_grads(slot, lambda c: start_gather(second, qgrad.at[slot], c))
 
         @pl.when(slot == 0)
         def _():
+            loads[1].wait()
             loads[2].wait()
+
+        make_terms(slot)
+
+        @pl.when(slot == 0)
+        def _():
             loads[3].wait()
-
-        make_terms(slot)
-
-        @pl.when(slot == 0)
-        def _():
-            loads[4].wait()
 
         own_block(qgrad.at[slot], wq)
 
@@ -369,18 +381,19 @@
             take_partner(second, wq, h - 1)
 
         take_partner(second, wq, chips - 1)
-        result = (gbuf[slot].astype(F32) + total[...]).astype(BF16)
-
-        @pl.when(slot == slots - 1)
-        def _():
-            grad_out[0] = result
-
-        @pl.when((slot < slots - 1) & (section > 0))
-        def _():
-            passed_buf[slot] = result
-            pass_copy(slot + 1).start()
-
-        finish_sum(slot)
+        for c in range(chunks):
+            result = (gbuf[slot, c].astype(F32) + total[:, part_of(c)]).astype(BF16)
+
+            @pl.when(slot == slots - 1)
+            def _():
+                grad_out[0, :, part_of(c)] = result
+
+            @pl.when((slot < slots - 1) & (section > 0))
+            def _():
+                passed_buf[slot, c] = result
+                pass_copy(slot + 1, c).start()
+
+    finish_sum(slots - 1)
 
     @pl.loop(0, slots)
     def _(slot):
@@ -401,7 +414,8 @@
 
         @pl.when((slot > 0) & (section > 0))
         def _():
-            pass_copy(slot).wait_send()
+            for c in range(chunks):
+                pass_copy(slot, c).wait_send()
             acc_copy(slot).wait_send()
 
 
@@ -413,6 +427,8 @@
         rows, width = grad_in.shape[1:]
         columns = queries.shape[3]
         chips = n_tp // 2
+        chunks = max(1, min(CHUNKS, width // LANES))
+        pieces = (chunks, rows, width // chunks)
         vmem = pl.BlockSpec(memory_space=pltpu.VMEM)
         hbm = pl.BlockSpec(memory_space=pl.ANY)
         block = (slots, chips, rows, width)
@@ -421,26 +437,26 @@
             pltpu.VMEM(wk.shape[1:], BF16),
             pltpu.VMEM(wv.shape[1:], BF16),
             pltpu.VMEM(wo.shape[1:], BF16),
-            pltpu.VMEM((slots, rows, width), BF16),
-            pltpu.VMEM((2 * slots, n_tp, rows, width), BF16),
-            pltpu.VMEM((slots, rows, columns), BF16),
+            pltpu.VMEM((slots, *pieces), BF16),
+            pltpu.VMEM((2 * slots, n_tp, *pieces), BF16),
+            pltpu.VMEM((slots, *pieces), BF16),
             pltpu.VMEM((rows, columns), BF16),
             pltpu.VMEM((rows, columns), BF16),
             pltpu.VMEM((rows, columns), F32),
-            pltpu.VMEM((slots, rows, width), BF16),
+            pltpu.VMEM((slots, *pieces), BF16),
             pltpu.VMEM((chips, rows, width), F32),
         ]
         scratch += [pltpu.VMEM(block, BF16)] * 6
         scratch += [pltpu.VMEM((slots, rows, width), BF16)] * 2
         dma = pltpu.SemaphoreType.DMA
         scratch += [
-            dma((5,)),
-            dma((2 * slots, chips, CHUNKS, 3)),
-            dma((2 * slots, n_tp, CHUNKS)),
+            dma((4 + chunks,)),
+            dma((2 * slots, chips, chunks, 3)),
+            dma((2 * slots, n_tp, chunks)),
             dma((2, slots, chips)),
             dma((2, slots, chips)),
             dma((2, slots, chips)),
-            dma((2, slots)),
+            dma((2, slots, chunks)),
             dma((2, slots)),
         ]
         return pl.pallas_call(

time: 87.8 us -> 86.8 us (0.989)
  Pallas kernels: 83.8 us -> 82.6 us
    pallas_call x1, Pallas kernels: 83.8 us -> 82.6 us  [body(): pl.pallas_call(functools.partial(kernel, n_sections, n_tp, slots), out_sh...]
where the time goes in v2:
time: 86.8 us; the launch traced here: 86.5 us
  Pallas kernels  82.6 us (95%)
  local copies, waits for them, and re-layouts  3.24 us (4%)
    pallas_call x1, Pallas kernels, body(): pl.pallas_call(functools.partial(kernel, n_sections, n_tp, slots), out_sh...  82.6 us
    unnamed x2, local copies, waits for them, and re-layouts  3.24 us

profile of v2, /device:TPU:0, one launch (start us, length us, event | category | flops | bytes accessed | tf_op | source)
XLA Modules:
  0.0 86.5 jit_solution(4230510884895133449)
XLA Ops:
  0.6 82.6 %shard_map.113 = (bf16[1,128,512]{2,1,0:T(8,128)(2,1)}, f32[1,128,512]{2,1,0:T(8,128)}) custom-call(bf16[1,128,512]{2,1,0:T(8,128)(2,1)} %grad_in.1, bf16[1,128,512]{2,1,0:T(8,128)(2,1)} %fresh.1, f32[1,128,512]{2,1,0:T(8,128)} %acc_in.1, bf16[1,2,128,512]{3,2,1,0:T(8,128)(2,1)} %queries.1, bf16[1,2,128,512]{3,2,1,0:T(8,128)(2,1)} %keys.1, ...), custom_call_target="tpu_custom_call" | custom-call | tf_op jit(solution)/shard_map/pallas_call | solution.py:462
  83.3 1.6 %copy.14 = bf16[1,128,512]{2,1,0:T(8,128)(2,1)} copy(bf16[1,128,512]{2,1,0:T(8,128)(2,1)} %get-tuple-element.4) | data formatting | bytes 262144
  84.9 1.7 %copy.15 = f32[1,128,512]{2,1,0:T(8,128)} copy(f32[1,128,512]{2,1,0:T(8,128)} %get-tuple-element.5) | data formatting | bytes 524288
